TPU v7x, 256 devices: a whole 4x4x8 slice. The times are simulated.
256 devices in a mesh: tm: 16 (over z, y_hi), obs: 16 (over x, y_lo, core).
Axes of the slice: x: 4, y: 4 (y_hi: 2, y_lo: 2; y = y_hi * 2 + y_lo), z: 8, core: 2. Of those that a mesh axis runs over, the one named last changes fastest.
Arguments:
- trajectory: bfloat16 [16, 256, 256, 128], P('tm', 'obs'), may hold values from -6 to 6
- weights: bfloat16 [8192, 128, 256], P(('tm', 'obs')), may hold values from -0.375 to 0.375
- observed: bfloat16 [8192, 128, 128], P(('tm', 'obs')), may hold values from -9 to 9
- window: int32 [8192, 1], P(('tm', 'obs')), may hold values from 0 to 15; in each aligned block of 32 rows (0 to 31, 32 to 63, ...) at most 4 rows name the same one
- block: int32 [8192], P(('tm', 'obs')), may hold values from 0 to 15
- counts: int32 [8192], P(('tm', 'obs')), may hold values from 32 to 128, as said below
- flags: int32 [8192, 128], P(('tm', 'obs')), may hold values 0 or 1
- inv_error: float32 [128], replicated, may hold values from 0.5 to 2
Outputs:
- departures: bfloat16 [8192, 128, 128], P(('tm', 'obs'))
- window_bias: float32 [16, 128], P('tm')
- window_chi: float32 [16, 128], P('tm')
Inputs may be any that keep to these rules, and one draw needn't show every extreme that they name: Among the 32 groups of one device, no sub-window is named by more than 4. `counts`: among the 32 groups of one device, one has all 128 slots live.
All inputs are finite; a program needn't handle non-finite values. No bound on the sum of `flags` on one device may be relied on, other than what follows from the above.
Results may differ from a plain program's by a relative error of at most 0.001.
Values may be sent and summed in bfloat16 or wider, within the bound.
A program may use at most 64 MiB of HBM per device.

v0:
```python
import functools

import jax
import jax.numpy as jnp
from jax import lax
from jax.sharding import Mesh
from jax.sharding import PartitionSpec as P

GCAP = 4
TM = ("tm_0", "tm_1")
TM_OBS = ("tm_0", "tm_1", "obs_0", "obs_1", "obs_2")
OBS = ("obs_0", "obs_1", "obs_2")


def one_axis_at_a_time(array, axes):
    return functools.reduce(lax.psum, axes, array)


def local_stats(picked, weights, observed, used, win_of, windows, inv_error):
    hx = jnp.einsum("gop,gpl->gol", weights, picked, preferred_element_type=jnp.float32)
    used_f = used.astype(jnp.float32)
    departure = used_f[:, :, None] * (observed.astype(jnp.float32) - hx) * inv_error[None, None, :]
    member = (win_of[:, None] == jnp.arange(windows, dtype=jnp.int32)[None, :]).astype(jnp.float32)
    sum_one = jnp.einsum(
        "gt,gl->tl", member, jnp.sum(departure, 1), precision=lax.Precision.HIGHEST
    )
    sum_two = jnp.einsum(
        "gt,gl->tl", member, jnp.sum(departure * departure, 1), precision=lax.Precision.HIGHEST
    )
    kept = jnp.einsum("gt,g->t", member, jnp.sum(used_f, 1), precision=lax.Precision.HIGHEST)
    return (departure.astype(jnp.bfloat16), sum_one, sum_two, kept)


def bucket_slots(win_of, groups, windows):
    member_int = (win_of[:, None] == jnp.arange(windows, dtype=jnp.int32)[None, :]).astype(
        jnp.int32
    )
    before = jnp.cumsum(member_int, 0) - member_int
    rank = jnp.sum(before * member_int, 1)
    slot_of = win_of * GCAP + rank
    table = (slot_of[None, :] == jnp.arange(windows * GCAP, dtype=jnp.int32)[:, None]).astype(
        jnp.int32
    )
    present = jnp.sum(table, 1) > 0
    source = jnp.sum(table * jnp.arange(groups, dtype=jnp.int32)[None, :], 1)
    return (slot_of, present, source)


def pick_own(sums, windows_axis_index):
    return tuple((lax.dynamic_slice_in_dim(item, windows_axis_index, 1, 0) for item in sums))


def per_device(trajectory, weights, observed, window, block, counts, flags, inv_error):
    groups = weights.shape[0]
    slots = weights.shape[1]
    windows = lax.axis_size(TM)
    win_of = window[:, 0]
    slot_ids = lax.broadcasted_iota(jnp.int32, (groups, slots), 1)
    used = jnp.where(slot_ids < counts[:, None], flags, 0)
    slot_of, present, source = bucket_slots(win_of, groups, windows)
    wanted = jnp.where(present, block[source], 0).reshape(windows, GCAP)
    local_slab = trajectory[0]
    found = local_slab[lax.all_to_all(wanted, TM, split_axis=0, concat_axis=0, tiled=True)]
    received = lax.all_to_all(found, TM, split_axis=0, concat_axis=0, tiled=True)
    received = received.reshape(windows * GCAP, local_slab.shape[1], local_slab.shape[2])
    picked = received[slot_of]
    departures, sum_one, sum_two, kept = local_stats(
        picked, weights, observed, used, win_of, windows, inv_error
    )
    sums = (
        one_axis_at_a_time(sum_one, TM_OBS),
        one_axis_at_a_time(sum_two, TM_OBS),
        one_axis_at_a_time(kept, TM_OBS),
    )
    sum_one, sum_two, kept = pick_own(sums, lax.axis_index(TM))
    window_bias = sum_one / jnp.sqrt(kept[:, None] + 1.0)
    window_chi = sum_two / (kept[:, None] + 1.0)
    return (departures, window_bias, window_chi)


def solution(mesh):
    finer = Mesh(mesh.devices.reshape(8, 2, 4, 2, 2), ("tm_0", "tm_1", "obs_0", "obs_1", "obs_2"))
    placed = (
        P(TM, OBS, None, None),
        P(TM_OBS, None, None),
        P(TM_OBS, None, None),
        P(TM_OBS, None),
        P(TM_OBS),
        P(TM_OBS),
        P(TM_OBS, None),
        P(),
    )
    return jax.shard_map(
        per_device,
        mesh=finer,
        in_specs=placed,
        out_specs=(P(TM_OBS, None, None), P(TM, None), P(TM, None)),
        check_vma=False,
    )
```

profile of v0, /device:TPU:1, one launch (start us, length us, event | category | flops | bytes accessed | tf_op | source)
XLA Modules:
  0.0 208.2 jit_solution(6675520321047817753)
XLA Ops:
  0.6 0.9 fusion.4
  1.6 0.8 select_reduce_fusion.1
  2.4 0.7 multiply_add_fusion
  3.1 0.1 convert_reduce_fusion
  3.2 1.4 gather_fusion
  4.7 20.4 %all_to_all.14 = s32[16,1,4]{2,1,0:T(1,128)S(1)} all-to-all(s32[16,1,4]{2,1,0:T(1,128)S(1)} %bitcast.39), channel_id=1, replica_groups=mesh['tm_0'=8,'tm_1'=2,'obs_0'=4,'obs_1'=2,'obs_2'=2] {'tm_0','tm_1'}, dimensions={0} | all-to-all | bytes 512 | tf_op jit(solution)/shard_map/all_to_all | solution.py:63
  25.2 0.1 copy.20
  25.3 0.1 reshape.111
  25.4 4.3 %gather_fusion.1 = bf16[64,256,128]{2,1,0:T(8,128)(2,1)} fusion(bf16[16,256,128]{2,1,0:T(8,128)(2,1)} %bitcast.37, s32[1024]{0:T(1024)S(1)} %pad_clamp_fusion.1), kind=kCustom, calls=%fused_computation.1 | custom fusion | bytes 8388864 | tf_op jit(solution)/shard_map/gather | solution.py:63
  29.7 4.7 %all-to-all-start.1 = ((bf16[16,4,256,128]{3,2,1,0:T(8,128)(2,1)}), bf16[16,4,256,128]{3,2,1,0:T(8,128)(2,1)}, u32[]{:S(2)}, u32[]{:S(2)}) async-start(bf16[16,4,256,128]{3,2,1,0:T(8,128)(2,1)} %bitcast.38), calls=%async_computation.1 | async-start | bytes 8388608 | tf_op jit(solution)/shard_map/all_to_all | solution.py:64
  34.4 0.2 fusion.11
  34.6 0.2 convolution_bitcast_fusion
  34.8 97.2 %all-to-all-done.1 = bf16[16,4,256,128]{3,2,1,0:T(8,128)(2,1)} async-done(((bf16[16,4,256,128]{3,2,1,0:T(8,128)(2,1)}), bf16[16,4,256,128]{3,2,1,0:T(8,128)(2,1)}, u32[]{:S(2)}, u32[]{:S(2)}) %all-to-all-start.1) | async-done | bytes 4194336 | tf_op jit(solution)/shard_map/all_to_all | solution.py:64
  132.1 4.4 %gather_fusion.2 = bf16[32,256,128]{2,1,0:T(8,128)(2,1)} fusion(bf16[64,256,128]{2,1,0:T(8,128)(2,1)} %bitcast.7, s32[1024]{0:T(1024)S(1)} %pad_clamp_fusion), kind=kCustom, calls=%fused_computation.2 | custom fusion | bytes 4194432 | tf_op jit(solution)/shard_map/gather | solution.py:66
  136.5 3.7 %multiply_reduce_fusion = (f32[32,128]{1,0:T(8,128)S(1)}, f32[32,128]{1,0:T(8,128)S(1)}, bf16[32,128,128]{2,1,0:T(8,128)(2,1)}) fusion(f32[128]{0:T(128)S(1)} %copy-done.5, bf16[32,128,256]{2,1,0:T(8,128)(2,1)S(1)} %copy-done, bf16[32,256,128]{2,1,0:T(8,128)(2,1)} %gather_fusion.2, bf16[32,128,128]{2,1,0:T(8,128)(2,1)S(1)} %copy-done.4, ...), kind=kOutput, calls=%fused_computation.6 | convolution fusion | flops 272621568 | bytes 6341120 | tf_op jit(solution)/shard_map/gop,gpl->gol/dot_general | solution.py:20
  140.2 0.3 fusion.2
  140.5 0.3 fusion.3
  140.7 21.6 %all-reduce = (f32[16,128]{1,0:T(8,128)S(1)}, f32[16]{0:T(128)S(1)}, f32[16,128]{1,0:T(8,128)S(1)}) all-reduce(f32[16,128]{1,0:T(8,128)S(1)} %fusion.3, f32[16]{0:T(128)S(1)} %convolution_bitcast_fusion, f32[16,128]{1,0:T(8,128)S(1)} %fusion.2), channel_id=1, replica_groups=mesh['tm_0'=8,'tm_1'=2,'obs_0'=4,'obs_1'=2,'obs_2'=2] {'tm_0'}, use_global_device_ids=true, to_apply=%region_5.6 | all-reduce | flops 4112 | bytes 32896 | tf_op jit(solution)/shard_map/psum | solution.py:16
  162.4 6.7 %all-reduce.4 = (f32[16,128]{1,0:T(8,128)S(1)}, f32[16]{0:T(128)S(1)}, f32[16,128]{1,0:T(8,128)S(1)}) all-reduce(f32[16,128]{1,0:T(8,128)S(1)} %get-tuple-element.7, f32[16]{0:T(128)S(1)} %get-tuple-element.8, f32[16,128]{1,0:T(8,128)S(1)} %get-tuple-element.9), channel_id=1, replica_groups=mesh['tm_0'=8,'tm_1'=2,'obs_0'=4,'obs_1'=2,'obs_2'=2] {'tm_1'}, use_global_device_ids=true, to_apply=%region_6.7 | all-reduce | flops 4112 | bytes 32896 | tf_op jit(solution)/shard_map/psum | solution.py:16
  169.0 13.2 %all-reduce.1 = (f32[16,128]{1,0:T(8,128)S(1)}, f32[16]{0:T(128)S(1)}, f32[16,128]{1,0:T(8,128)S(1)}) all-reduce(f32[16,128]{1,0:T(8,128)S(1)} %get-tuple-element.19, f32[16]{0:T(128)S(1)} %get-tuple-element.20, f32[16,128]{1,0:T(8,128)S(1)} %get-tuple-element.21), channel_id=1, replica_groups=mesh['tm_0'=8,'tm_1'=2,'obs_0'=4,'obs_1'=2,'obs_2'=2] {'obs_0'}, use_global_device_ids=true, to_apply=%region_7.8 | all-reduce | flops 4112 | bytes 32896 | tf_op jit(solution)/shard_map/psum | solution.py:16
  182.2 5.7 %all-reduce.3 = (f32[16,128]{1,0:T(8,128)S(1)}, f32[16]{0:T(128)S(1)}, f32[16,128]{1,0:T(8,128)S(1)}) all-reduce(f32[16,128]{1,0:T(8,128)S(1)} %get-tuple-element.10, f32[16]{0:T(128)S(1)} %get-tuple-element.11, f32[16,128]{1,0:T(8,128)S(1)} %get-tuple-element.12), channel_id=1, replica_groups=mesh['tm_0'=8,'tm_1'=2,'obs_0'=4,'obs_1'=2,'obs_2'=2] {'obs_1'}, use_global_device_ids=true, to_apply=%region_8.9 | all-reduce | flops 4112 | bytes 32896 | tf_op jit(solution)/shard_map/psum | solution.py:16
  187.9 18.4 %all-reduce.2 = (f32[16,128]{1,0:T(8,128)S(1)}, f32[16]{0:T(128)S(1)}, f32[16,128]{1,0:T(8,128)S(1)}) all-reduce(f32[16,128]{1,0:T(8,128)S(1)} %get-tuple-element.16, f32[16]{0:T(128)S(1)} %get-tuple-element.17, f32[16,128]{1,0:T(8,128)S(1)} %get-tuple-element.18), channel_id=1, replica_groups=mesh['tm_0'=8,'tm_1'=2,'obs_0'=4,'obs_1'=2,'obs_2'=2] {'obs_2'}, use_global_device_ids=true, to_apply=%region_9.10 | all-reduce | flops 4112 | bytes 32896 | tf_op jit(solution)/shard_map/psum | solution.py:16
  206.3 0.6 dynamic_slice.10
  207.6 0.5 dynamic-slice_divide_fusion
  (22 shorter events, 0.3 us)
Async XLA Ops:
  0.6 135.9 %copy-start = (bf16[32,128,256]{2,1,0:T(8,128)(2,1)S(1)}, bf16[32,128,256]{2,1,0:T(8,128)(2,1)}, u32[]{:S(2)}) copy-start(bf16[32,128,256]{2,1,0:T(8,128)(2,1)} %param.9) | copy-start | bytes 6291460
  29.7 4.7 %copy-start.2 = (s32[32,1]{0,1:T(1,128)S(1)}, s32[32,1]{0,1:T(1,128)}, u32[]{:S(2)}) copy-start(s32[32,1]{0,1:T(1,128)} %param.11) | copy-start | bytes 388
  29.7 4.7 %copy-start.1 = (s32[32,128]{1,0:T(8,128)S(1)}, s32[32,128]{1,0:T(8,128)}, u32[]{:S(2)}) copy-start(s32[32,128]{1,0:T(8,128)} %param.14) | copy-start | bytes 49156
  29.7 4.7 %copy-start.3 = (s32[32]{0:T(128)S(1)}, s32[32]{0:T(128)}, u32[]{:S(2)}) copy-start(s32[32]{0:T(128)} %param.13) | copy-start | bytes 388
  29.7 102.4 %all-to-all-start.1 = ((bf16[16,4,256,128]{3,2,1,0:T(8,128)(2,1)}), bf16[16,4,256,128]{3,2,1,0:T(8,128)(2,1)}, u32[]{:S(2)}, u32[]{:S(2)}) async-start(bf16[16,4,256,128]{3,2,1,0:T(8,128)(2,1)} %bitcast.38), calls=%async_computation.1 | async-start | bytes 8388608 | tf_op jit(solution)/shard_map/all_to_all | solution.py:64
  132.1 4.4 %copy-start.4 = (bf16[32,128,128]{2,1,0:T(8,128)(2,1)S(1)}, bf16[32,128,128]{2,1,0:T(8,128)(2,1)}, u32[]{:S(2)}) copy-start(bf16[32,128,128]{2,1,0:T(8,128)(2,1)} %param.10) | copy-start | bytes 3145732
  132.1 4.4 %copy-start.5 = (f32[128]{0:T(128)S(1)}, f32[128]{0:T(128)}, u32[]{:S(2)}) copy-start(f32[128]{0:T(128)} %param.15) | copy-start | bytes 1540
where the time goes:
time: 209 us; the launch traced here: 208 us
  waiting for transfers between devices  97.2 us (47%)
  blocking collectives  86 us (41%)
  local copies, waits for them, and re-layouts  11.1 us (5%)
  starting transfers between devices  4.66 us (2%)
  matrix products  4.42 us (2%)
  other arithmetic  3.28 us (2%)
    all_to_all x1, waiting for transfers between devices, per_device(): lax.all_to_all(found, TM, split_axis=0, concat_axis=0, tiled=True)  97.2 us
    psum x5, blocking collectives, one_axis_at_a_time(): return functools.reduce(lax.psum, axes, array)  65.6 us
    all_to_all x1, blocking collectives, per_device(): lax.all_to_all(wanted, TM, split_axis=0, concat_axis=0, tiled=True)  20.4 us
    all_to_all x1, starting transfers between devices, per_device(): lax.all_to_all(found, TM, split_axis=0, concat_axis=0, tiled=True)  4.66 us
    gather x1, local copies, waits for them, and re-layouts, per_device(): picked = received[slot_of]  4.42 us
    gather x1, local copies, waits for them, and re-layouts, per_device(): local_slab[lax.all_to_all(wanted, TM, split_axis=0, concat_axis=0, tiled=...  4.28 us
  transfers between devices with their start and end apart: 1, of which 1 were waited for; matrix products, arithmetic and copies ran while one was open for 0% of the time, Pallas kernels for 0%

commit v1 on v0

v1 whole, which is shorter than its diff:
```python
import jax
import jax.numpy as jnp
from jax import lax
from jax.experimental import pallas as pl
from jax.experimental.pallas import tpu as pltpu
from jax.sharding import PartitionSpec as P

MESH = pl.DeviceIdType.MESH
GCAP = 4
PIECE = 2

SLABS = ((0, 0), (-1, 0), (1, 0), (-2, 0), (2, 0))
TABLE_TO = ((0, 1), (-1, 0), (-1, 1), (-2, 0), (1, 0), (1, 1), (2, 1))
PICKS = (
    (0, 1, 0, 0),
    (0, 1, 1, 0),
    (0, 1, 2, 0),
    (0, 1, 3, 0),
    (0, 1, 4, 0),
    (1, 0, 3, 1),
    (1, 1, 3, 2),
    (2, 0, 3, 3),
    (-1, 0, 4, 4),
    (-1, 1, 4, 5),
    (-2, 1, 4, 6),
)


def kernel(
    traj, weights, observed, window, block, counts, flags, inv,
    dep_out, bias_out, chi_out,
    s0, s1, s2, s3, s4, picked, outgoing, w_all, y_all, deps, dep_rows, used_t, my_table, tables,
    parts, from_tm, row_sum, from_obs, my_smem, far_smem,
    load_sem, slab_send, slab_recv, pick_send, pick_recv, table_send, table_recv,
    tm_send, tm_recv, obs_send, obs_recv, out_sem,
):
    slabs = (s0, s1, s2, s3, s4)
    tm = lax.axis_index("tm")
    obs = lax.axis_index("obs")
    z, y = tm // 2, lax.rem(tm, 2)
    n_tm, n_obs = 16, 16
    groups = 32

    def at(dz, dy):
        return lax.rem(z + dz + 8, 8) * 2 + (1 - y if dy else y)

    loads = [
        pltpu.make_async_copy(traj.at[0], s0, load_sem.at[0]),
        pltpu.make_async_copy(weights, w_all, load_sem.at[1]),
        pltpu.make_async_copy(observed, y_all, load_sem.at[2]),
    ]
    for load in loads:
        load.start()

    barrier = pltpu.get_barrier_semaphore()

    def greet(step, carry):
        pl.semaphore_signal(
            barrier, 1, device_id={"tm": lax.rem(tm + step, n_tm)}, device_id_type=MESH
        )
        pl.semaphore_signal(
            barrier, 1, device_id={"obs": lax.rem(obs + step, n_obs)}, device_id_type=MESH
        )
        return carry

    lax.fori_loop(1, 16, greet, 0)

    lane = lax.broadcasted_iota(jnp.int32, (groups, 128), 1)
    row = lax.broadcasted_iota(jnp.int32, (groups, 128), 0)
    win_col = jnp.broadcast_to(window[...], (groups, 128))
    diag = lane == row
    win_row = jnp.sum(jnp.where(diag, win_col, 0), 0, keepdims=True)
    same = win_col == win_row
    rank_row = jnp.sum(jnp.where(same & (row < lane), 1, 0), 0, keepdims=True)
    slot_row = win_row * GCAP + rank_row
    rank_col = jnp.sum(jnp.where(same & (lane < row), 1, 0), 1, keepdims=True)
    slot_col = window[...] * GCAP + rank_col
    hit = slot_col == lane
    block_row = block[...]
    block_col = jnp.sum(
        jnp.where(diag, jnp.broadcast_to(block_row, (groups, 128)), 0), 1, keepdims=True
    )
    my_table[0:1, :] = jnp.sum(jnp.where(hit, block_col, 0), 0, keepdims=True)
    my_table[1:2, :] = jnp.sum(jnp.where(hit, row + 1, 0), 0, keepdims=True) - 1
    my_table[2:3, :] = slot_row
    count_col = jnp.sum(
        jnp.where(diag, jnp.broadcast_to(counts[...], (groups, 128)), 0), 1, keepdims=True
    )
    used = jnp.where(lane < count_col, flags[...], 0).astype(jnp.float32)
    used_t[...] = jnp.transpose(used).astype(jnp.bfloat16)

    loads[0].wait()
    pl.semaphore_wait(barrier, 2 * 15)

    pieces = 16 // PIECE

    def slab_copy(flow, piece):
        source, target, dz = ((s0, s1, 1), (s0, s2, -1), (s1, s3, 1), (s2, s4, -1))[flow]
        span = pl.ds(piece * PIECE, PIECE)
        return pltpu.make_async_remote_copy(
            src_ref=source.at[span], dst_ref=target.at[span],
            send_sem=slab_send.at[flow, piece], recv_sem=slab_recv.at[flow, piece],
            device_id={"tm": at(dz, 0)}, device_id_type=MESH,
        )

    def table_copy(k):
        return pltpu.make_async_remote_copy(
            src_ref=my_table, dst_ref=tables.at[k],
            send_sem=table_send.at[k], recv_sem=table_recv.at[k],
            device_id={"tm": at(*TABLE_TO[k])}, device_id_type=MESH,
        )

    for k in range(len(TABLE_TO)):
        table_copy(k).start()
    for piece in range(pieces):
        slab_copy(0, piece).start()
        slab_copy(1, piece).start()

    to_smem = pltpu.make_async_copy(my_table, my_smem, load_sem.at[3])
    to_smem.start()
    for k in range(len(TABLE_TO)):
        table_copy(k).wait_recv()
    far_to_smem = pltpu.make_async_copy(tables, far_smem, load_sem.at[4])
    far_to_smem.start()
    to_smem.wait()
    far_to_smem.wait()

    def pick_copy(m):
        dz, dy, _, _ = PICKS[m]
        return pltpu.make_async_remote_copy(
            src_ref=outgoing.at[m], dst_ref=picked.at[m],
            send_sem=pick_send.at[m], recv_sem=pick_recv.at[m],
            device_id={"tm": at(dz, dy)}, device_id_type=MESH,
        )

    def pick(*numbers):
        for m in numbers:
            _, _, slab, k = PICKS[m]
            first = at(*SLABS[slab]) * GCAP
            for r in range(GCAP):
                outgoing[m, r] = slabs[slab][far_smem[k, 0, first + r]]
        for m in numbers:
            pick_copy(m).start()

    inv_row = inv[...]
    group_ids = lax.broadcasted_iota(jnp.int32, (groups, 128), 0)
    done = []

    def part_copy(q, dz, dy):
        return pltpu.make_async_remote_copy(
            src_ref=parts.at[q], dst_ref=from_tm.at[q],
            send_sem=tm_send.at[q], recv_sem=tm_recv.at[q],
            device_id={"tm": at(dz, dy)}, device_id_type=MESH,
        )

    def send_part():
        q, dz, dy = done[-1]
        if q > 0:
            part_copy(q, dz, dy).start()

    def compute(dz, dy, block_of):
        q = len(done)
        first = at(dz, dy) * GCAP

        def body(r, carry):
            one, two, kept = carry
            group = my_smem[1, first + r]
            place = jnp.maximum(group, 0)
            chosen = jnp.where(group_ids == group, 1.0, 0.0).astype(jnp.bfloat16)
            mask = jnp.dot(used_t[...], chosen, preferred_element_type=jnp.float32)
            hx = jnp.dot(
                w_all[place], block_of(r, my_smem[0, first + r]), preferred_element_type=jnp.float32
            )
            departure = mask * (y_all[place].astype(jnp.float32) - hx) * inv_row
            deps[first + r] = departure.astype(jnp.bfloat16)
            one = one + jnp.sum(departure.reshape(16, 8, 128), 0)
            two = two + jnp.sum((departure * departure).reshape(16, 8, 128), 0)
            kept = kept + jnp.sum(mask.reshape(16, 8, 128), 0)
            return one, two, kept

        zero = jnp.zeros((8, 128), jnp.float32)
        one, two, kept = lax.fori_loop(0, GCAP, body, (zero, zero, zero))
        parts[q, 0:1, :] = jnp.sum(one, 0, keepdims=True)
        parts[q, 1:2, :] = jnp.sum(two, 0, keepdims=True)
        parts[q, 2:3, :] = jnp.sum(kept, 0, keepdims=True)
        if done:
            send_part()
        done.append((q, dz, dy))

    def compute_slab(slab):
        dz, dy = SLABS[slab]
        compute(dz, dy, lambda r, number: slabs[slab][number])

    def compute_picked(m):
        dz, dy, slab, _ = PICKS[m]
        compute(SLABS[slab][0] - dz, dy, lambda r, number: picked[m, r])

    pick(0)
    loads[1].wait()
    loads[2].wait()
    parts[...] = jnp.zeros_like(parts)
    compute_slab(0)

    for piece in range(pieces):
        slab_copy(0, piece).wait_recv()
        slab_copy(2, piece).start()
        slab_copy(1, piece).wait_recv()
        slab_copy(3, piece).start()
    pick(1, 2)
    pick_copy(0).wait_recv()
    compute_picked(0)
    compute_slab(1)
    compute_slab(2)
    pick_copy(1).wait_recv()
    compute_picked(1)
    pick_copy(2).wait_recv()
    compute_picked(2)

    for piece in range(pieces):
        slab_copy(2, piece).wait_recv()
        slab_copy(3, piece).wait_recv()
    pick(6, 9, 7, 10, 5, 8)
    pick(3, 4)
    compute_slab(3)
    compute_slab(4)
    for m in (6, 9, 7, 10, 5, 8, 3, 4):
        pick_copy(m).wait_recv()
        compute_picked(m)

    def put(lo, hi):
        for g in range(lo, hi):
            dep_rows[g] = deps[my_smem[2, g]]

    def out_copy(lo, size):
        span = pl.ds(lo, size)
        return pltpu.make_async_copy(dep_rows.at[span], dep_out.at[span], out_sem.at[lo // size])

    put(0, 4)
    send_part()
    put(4, 16)
    out_copy(0, 16).start()
    total = parts[0]
    for q, dz, dy in done[1:]:
        part_copy(q, dz, dy).wait_recv()
        total = total + from_tm[q]
    row_sum[...] = total
    put(16, 20)

    def obs_copy(step):
        return pltpu.make_async_remote_copy(
            src_ref=row_sum, dst_ref=from_obs.at[step],
            send_sem=obs_send.at[step], recv_sem=obs_recv.at[step],
            device_id={"obs": lax.rem(obs + step, n_obs)}, device_id_type=MESH,
        )

    for step in range(1, n_obs):
        obs_copy(step).start()
    put(20, 32)
    out_copy(16, 16).start()

    for piece in range(pieces):
        for flow in range(4):
            slab_copy(flow, piece).wait_send()
    for k in range(len(TABLE_TO)):
        table_copy(k).wait_send()
    for m in range(len(PICKS)):
        pick_copy(m).wait_send()
    for q, dz, dy in done[1:]:
        part_copy(q, dz, dy).wait_send()

    for step in range(1, n_obs):
        obs_copy(step).wait_recv()
        total = total + from_obs[step]
    plus_one = total[2:3, :] + 1.0
    bias_out[...] = total[0:1, :] / jnp.sqrt(plus_one)
    chi_out[...] = total[1:2, :] / plus_one
    for step in range(1, n_obs):
        obs_copy(step).wait_send()
    out_copy(0, 16).wait()
    out_copy(16, 16).wait()


def per_device(trajectory, weights, observed, window, block, counts, flags, inv_error):
    groups, slots, columns = weights.shape
    levels = observed.shape[2]
    blocks = trajectory.shape[1]
    bf16, f32, i32 = jnp.bfloat16, jnp.float32, jnp.int32
    pad = ((0, 0), (0, 128 - groups))
    block = jnp.pad(block.reshape(1, groups), pad)
    counts = jnp.pad(counts.reshape(1, groups), pad)
    dma = pltpu.SemaphoreType.DMA
    pieces = blocks // PIECE
    picks, tables = len(PICKS), len(TABLE_TO)
    any_space = pl.BlockSpec(memory_space=pl.ANY)
    hbm = pl.BlockSpec(memory_space=pltpu.HBM)
    vmem = pl.BlockSpec(memory_space=pltpu.VMEM)
    slab = pltpu.VMEM((blocks, columns, levels), bf16)
    return pl.pallas_call(
        kernel,
        out_shape=(
            jax.ShapeDtypeStruct((groups, slots, levels), bf16),
            jax.ShapeDtypeStruct((1, levels), f32),
            jax.ShapeDtypeStruct((1, levels), f32),
        ),
        in_specs=[hbm] * 3 + [vmem] * 5,
        out_specs=(any_space, vmem, vmem),
        scratch_shapes=[
            slab, slab, slab, slab, slab,
            pltpu.VMEM((picks, GCAP, columns, levels), bf16),
            pltpu.VMEM((picks, GCAP, columns, levels), bf16),
            pltpu.VMEM((groups, slots, columns), bf16),
            pltpu.VMEM((groups, slots, levels), bf16),
            pltpu.VMEM((16 * GCAP, slots, levels), bf16),
            pltpu.VMEM((groups, slots, levels), bf16),
            pltpu.VMEM((slots, groups), bf16),
            pltpu.VMEM((8, 128), i32),
            pltpu.VMEM((tables, 8, 128), i32),
            pltpu.VMEM((16, 8, levels), f32),
            pltpu.VMEM((16, 8, levels), f32),
            pltpu.VMEM((8, levels), f32),
            pltpu.VMEM((16, 8, levels), f32),
            pltpu.SMEM((8, 128), i32),
            pltpu.SMEM((tables, 8, 128), i32),
            dma((5,)),
            dma((4, pieces)), dma((4, pieces)),
            dma((picks,)), dma((picks,)),
            dma((tables,)), dma((tables,)),
            dma((16,)), dma((16,)),
            dma((16,)), dma((16,)),
            dma((2,)),
        ],
        compiler_params=pltpu.CompilerParams(
            collective_id=0, has_side_effects=True, vmem_limit_bytes=48 * 2**20
        ),
        name="exchange_and_check",
    )(
        trajectory, weights, observed, window, block, counts, flags,
        inv_error.reshape(1, levels),
    )


def solution(mesh):
    both = ("tm", "obs")
    return jax.shard_map(
        per_device,
        mesh=mesh,
        in_specs=(
            P("tm", "obs", None, None),
            P(both, None, None),
            P(both, None, None),
            P(both, None),
            P(both),
            P(both),
            P(both, None),
            P(),
        ),
        out_specs=(P(both, None, None), P("tm", None), P("tm", None)),
        check_vma=False,
    )
```

time: 209 us -> 111 us (0.53)
  Pallas kernels: 0 us -> 100 us
  waiting for transfers between devices: 97.2 us -> 0 us
  blocking collectives: 86 us -> 0 us
  starting transfers between devices: 4.66 us -> 0 us
  matrix products: 4.42 us -> 0 us
  other arithmetic: 3.28 us -> 0 us
    pallas_call x0 -> x1, Pallas kernels: none -> 100 us  [per_device(): pl.pallas_call(kernel, out_shape=(jax.ShapeDtypeStruct((groups, slots, le...]
    all_to_all x1 -> x0, waiting for transfers between devices: 97.2 us -> none  [per_device(): lax.all_to_all(found, TM, split_axis=0, concat_axis=0, tiled=True)]
    psum x5 -> x0, blocking collectives: 65.6 us -> none  [one_axis_at_a_time(): return functools.reduce(lax.psum, axes, array)]
    all_to_all x1 -> x0, blocking collectives: 20.4 us -> none  [per_device(): lax.all_to_all(wanted, TM, split_axis=0, concat_axis=0, tiled=True)]
    gather x3 -> x0, local copies, waits for them, and re-layouts: 10.1 us -> none  [the longest x1 4.42 us: per_device(): picked = received[slot_of]]
    unnamed x12 -> x14, local copies, waits for them, and re-layouts: 0.03 us -> 8.14 us
    all_to_all x1 -> x0, starting transfers between devices: 4.66 us -> none  [per_device(): lax.all_to_all(found, TM, split_axis=0, concat_axis=0, tiled=True)]
    dot_general x4 -> x0, matrix products: 4.42 us -> none  [the longest x1 3.72 us: local_stats(): jnp.einsum('gop,gpl->gol', weights, picked, preferred_element_type=jnp.fl...]
  transfers between devices with their start and end apart: 1 -> 0, of which waited for: 1 -> 0; matrix products, arithmetic and copies ran while one was open for 0% -> 0% of each run, Pallas kernels for 0% -> 0%
where the time goes in v1:
time: 111 us; the launch traced here: 110 us
  Pallas kernels  100 us (90%)
  local copies, waits for them, and re-layouts  9.46 us (9%)
    pallas_call x1, Pallas kernels, per_device(): pl.pallas_call(kernel, out_shape=(jax.ShapeDtypeStruct((groups, slots, le...  100 us
    unnamed x14, local copies, waits for them, and re-layouts  8.14 us

profile of v1, /device:TPU:1, one launch (start us, length us, event | category | flops | bytes accessed | tf_op | source)
XLA Modules:
  0.0 110.3 jit_solution(3314060804839038730)
XLA Ops:
  0.6 0.7 pad.7.block
  1.3 0.7 pad.8.counts
  2.0 0.7 copy.11.window
  2.7 0.0 copy-start
  2.7 1.6 %copy-done = bf16[32,128,256]{2,1,0:T(8,128)(2,1)S(1)} copy-done((bf16[32,128,256]{2,1,0:T(8,128)(2,1)S(1)}, bf16[32,128,256]{2,1,0:T(8,128)(2,1)}, u32[]{:S(2)}) %copy-start) | copy-done | bytes 2097176
  4.3 0.0 copy-start.1
  4.3 1.2 %copy-done.1 = bf16[1,16,256,128]{3,2,1,0:T(8,128)(2,1)S(1)} copy-done((bf16[1,16,256,128]{3,2,1,0:T(8,128)(2,1)S(1)}, bf16[1,16,256,128]{3,2,1,0:T(8,128)(2,1)}, u32[]{:S(2)}) %copy-start.1) | copy-done | bytes 1048600
  5.5 0.0 copy-start.2
  5.5 1.2 %copy-done.2 = bf16[32,128,128]{2,1,0:T(8,128)(2,1)S(1)} copy-done((bf16[32,128,128]{2,1,0:T(8,128)(2,1)S(1)}, bf16[32,128,128]{2,1,0:T(8,128)(2,1)}, u32[]{:S(2)}) %copy-start.2) | copy-done | bytes 1048600
  6.7 0.0 copy-start.3
  6.7 0.7 copy-done.3
  7.4 0.0 copy-start.4
  7.4 0.7 copy-done.4
  8.1 100.2 %exchange_and_check.1 = (bf16[32,128,128]{2,1,0:T(8,128)(2,1)S(1)}, f32[1,128]{1,0:T(1,128)S(1)}, f32[1,128]{1,0:T(1,128)S(1)}) custom-call(bf16[1,16,256,128]{3,2,1,0:T(8,128)(2,1)S(1)} %copy-done.1, bf16[32,128,256]{2,1,0:T(8,128)(2,1)S(1)} %copy-done, bf16[32,128,128]{2,1,0:T(8,128)(2,1)S(1)} %copy-done.2, s32[32,1]{1,0:T(8,128)S(1)} %copy.11.window, ...), custom_call_target="tpu_custom_call" | custom-call | tf_op jit(solution)/shard_map/exchange_and_check/pallas_call | solution.py:298
  108.3 1.0 copy.15
  109.3 0.5 copy.16
  109.8 0.5 copy.17
Async XLA Ops:
  2.7 1.6 %copy-start = (bf16[32,128,256]{2,1,0:T(8,128)(2,1)S(1)}, bf16[32,128,256]{2,1,0:T(8,128)(2,1)}, u32[]{:S(2)}) copy-start(bf16[32,128,256]{2,1,0:T(8,128)(2,1)} %weights.1) | copy-start | bytes 6291460
  4.3 1.2 %copy-start.1 = (bf16[1,16,256,128]{3,2,1,0:T(8,128)(2,1)S(1)}, bf16[1,16,256,128]{3,2,1,0:T(8,128)(2,1)}, u32[]{:S(2)}) copy-start(bf16[1,16,256,128]{3,2,1,0:T(8,128)(2,1)} %traj.1) | copy-start | bytes 3145732
  5.5 1.2 %copy-start.2 = (bf16[32,128,128]{2,1,0:T(8,128)(2,1)S(1)}, bf16[32,128,128]{2,1,0:T(8,128)(2,1)}, u32[]{:S(2)}) copy-start(bf16[32,128,128]{2,1,0:T(8,128)(2,1)} %observed.1) | copy-start | bytes 3145732
  6.7 0.7 copy-start.3
  7.4 0.7 copy-start.4

commit v2 on v1

--- a/solution.py
+++ b/solution.py
@@ -28,8 +28,9 @@
 
 def kernel(
     traj, weights, observed, window, block, counts, flags, inv,
-    dep_out, bias_out, chi_out,
-    s0, s1, s2, s3, s4, picked, outgoing, w_all, y_all, deps, dep_rows, used_t, my_table, tables,
+    dep_out, sums_out,
+    s0, s1, s2, s3, s4, picked, outgoing, w_all, y_all, deps, dep_rows, used_t,
+    win_row, block_row, count_row, flag_rows, inv_vmem, my_table, tables,
     parts, from_tm, row_sum, from_obs, my_smem, far_smem,
     load_sem, slab_send, slab_recv, pick_send, pick_recv, table_send, table_recv,
     tm_send, tm_recv, obs_send, obs_recv, out_sem,
@@ -44,14 +45,6 @@
     def at(dz, dy):
         return lax.rem(z + dz + 8, 8) * 2 + (1 - y if dy else y)
 
-    loads = [
-        pltpu.make_async_copy(traj.at[0], s0, load_sem.at[0]),
-        pltpu.make_async_copy(weights, w_all, load_sem.at[1]),
-        pltpu.make_async_copy(observed, y_all, load_sem.at[2]),
-    ]
-    for load in loads:
-        load.start()
-
     barrier = pltpu.get_barrier_semaphore()
 
     def greet(step, carry):
@@ -65,28 +58,37 @@
 
     lax.fori_loop(1, 16, greet, 0)
 
-    lane = lax.broadcasted_iota(jnp.int32, (groups, 128), 1)
-    row = lax.broadcasted_iota(jnp.int32, (groups, 128), 0)
-    win_col = jnp.broadcast_to(window[...], (groups, 128))
+    pairs = (
+        (traj.at[0], s0), (weights, w_all), (observed, y_all), (window, win_row), (block, block_row),
+        (counts, count_row), (flags, flag_rows), (inv, inv_vmem),
+    )
+    loads = [
+        pltpu.make_async_copy(source, target, load_sem.at[n])
+        for n, (source, target) in enumerate(pairs)
+    ]
+    for load in loads[3:] + loads[:3]:
+        load.start()
+
+    for load in loads[3:]:
+        load.wait()
+    lane = lax.broadcasted_iota(jnp.int32, (groups, groups), 1)
+    row = lax.broadcasted_iota(jnp.int32, (groups, groups), 0)
     diag = lane == row
-    win_row = jnp.sum(jnp.where(diag, win_col, 0), 0, keepdims=True)
-    same = win_col == win_row
+
+    def turned(ref):
+        return jnp.sum(jnp.where(diag, ref[...], 0), 1, keepdims=True)
+
+    same = turned(win_row) == win_row[...]
     rank_row = jnp.sum(jnp.where(same & (row < lane), 1, 0), 0, keepdims=True)
-    slot_row = win_row * GCAP + rank_row
     rank_col = jnp.sum(jnp.where(same & (lane < row), 1, 0), 1, keepdims=True)
-    slot_col = window[...] * GCAP + rank_col
-    hit = slot_col == lane
-    block_row = block[...]
-    block_col = jnp.sum(
-        jnp.where(diag, jnp.broadcast_to(block_row, (groups, 128)), 0), 1, keepdims=True
-    )
-    my_table[0:1, :] = jnp.sum(jnp.where(hit, block_col, 0), 0, keepdims=True)
-    my_table[1:2, :] = jnp.sum(jnp.where(hit, row + 1, 0), 0, keepdims=True) - 1
-    my_table[2:3, :] = slot_row
-    count_col = jnp.sum(
-        jnp.where(diag, jnp.broadcast_to(counts[...], (groups, 128)), 0), 1, keepdims=True
-    )
-    used = jnp.where(lane < count_col, flags[...], 0).astype(jnp.float32)
+    wide_lane = lax.broadcasted_iota(jnp.int32, (groups, 128), 1)
+    wide_row = lax.broadcasted_iota(jnp.int32, (groups, 128), 0)
+    hit = turned(win_row) * GCAP + rank_col == wide_lane
+    my_table[...] = jnp.zeros_like(my_table)
+    my_table[0:1, :] = jnp.sum(jnp.where(hit, turned(block_row), 0), 0, keepdims=True)
+    my_table[1:2, :] = jnp.sum(jnp.where(hit, wide_row + 1, 0), 0, keepdims=True) - 1
+    my_table[2:3, 0:groups] = win_row[...] * GCAP + rank_row
+    used = jnp.where(wide_lane < turned(count_row), flag_rows[...], 0).astype(jnp.float32)
     used_t[...] = jnp.transpose(used).astype(jnp.bfloat16)
 
     loads[0].wait()
@@ -116,11 +118,11 @@
         slab_copy(0, piece).start()
         slab_copy(1, piece).start()
 
-    to_smem = pltpu.make_async_copy(my_table, my_smem, load_sem.at[3])
+    to_smem = pltpu.make_async_copy(my_table, my_smem, load_sem.at[8])
     to_smem.start()
     for k in range(len(TABLE_TO)):
         table_copy(k).wait_recv()
-    far_to_smem = pltpu.make_async_copy(tables, far_smem, load_sem.at[4])
+    far_to_smem = pltpu.make_async_copy(tables, far_smem, load_sem.at[9])
     far_to_smem.start()
     to_smem.wait()
     far_to_smem.wait()
@@ -142,7 +144,7 @@
         for m in numbers:
             pick_copy(m).start()
 
-    inv_row = inv[...]
+    inv_row = inv_vmem[...]
     group_ids = lax.broadcasted_iota(jnp.int32, (groups, 128), 0)
     done = []
 
@@ -271,9 +273,7 @@
     for step in range(1, n_obs):
         obs_copy(step).wait_recv()
         total = total + from_obs[step]
-    plus_one = total[2:3, :] + 1.0
-    bias_out[...] = total[0:1, :] / jnp.sqrt(plus_one)
-    chi_out[...] = total[1:2, :] / plus_one
+    sums_out[...] = total
     for step in range(1, n_obs):
         obs_copy(step).wait_send()
     out_copy(0, 16).wait()
@@ -285,25 +285,20 @@
     levels = observed.shape[2]
     blocks = trajectory.shape[1]
     bf16, f32, i32 = jnp.bfloat16, jnp.float32, jnp.int32
-    pad = ((0, 0), (0, 128 - groups))
-    block = jnp.pad(block.reshape(1, groups), pad)
-    counts = jnp.pad(counts.reshape(1, groups), pad)
     dma = pltpu.SemaphoreType.DMA
     pieces = blocks // PIECE
     picks, tables = len(PICKS), len(TABLE_TO)
     any_space = pl.BlockSpec(memory_space=pl.ANY)
-    hbm = pl.BlockSpec(memory_space=pltpu.HBM)
     vmem = pl.BlockSpec(memory_space=pltpu.VMEM)
     slab = pltpu.VMEM((blocks, columns, levels), bf16)
-    return pl.pallas_call(
+    departures, sums = pl.pallas_call(
         kernel,
         out_shape=(
             jax.ShapeDtypeStruct((groups, slots, levels), bf16),
-            jax.ShapeDtypeStruct((1, levels), f32),
-            jax.ShapeDtypeStruct((1, levels), f32),
+            jax.ShapeDtypeStruct((8, levels), f32),
         ),
-        in_specs=[hbm] * 3 + [vmem] * 5,
-        out_specs=(any_space, vmem, vmem),
+        in_specs=[any_space] * 8,
+        out_specs=(any_space, vmem),
         scratch_shapes=[
             slab, slab, slab, slab, slab,
             pltpu.VMEM((picks, GCAP, columns, levels), bf16),
@@ -313,6 +308,11 @@
             pltpu.VMEM((16 * GCAP, slots, levels), bf16),
             pltpu.VMEM((groups, slots, levels), bf16),
             pltpu.VMEM((slots, groups), bf16),
+            pltpu.VMEM((1, groups), i32),
+            pltpu.VMEM((1, groups), i32),
+            pltpu.VMEM((1, groups), i32),
+            pltpu.VMEM((groups, slots), i32),
+            pltpu.VMEM((1, levels), f32),
             pltpu.VMEM((8, 128), i32),
             pltpu.VMEM((tables, 8, 128), i32),
             pltpu.VMEM((16, 8, levels), f32),
@@ -321,7 +321,7 @@
             pltpu.VMEM((16, 8, levels), f32),
             pltpu.SMEM((8, 128), i32),
             pltpu.SMEM((tables, 8, 128), i32),
-            dma((5,)),
+            dma((10,)),
             dma((4, pieces)), dma((4, pieces)),
             dma((picks,)), dma((picks,)),
             dma((tables,)), dma((tables,)),
@@ -330,13 +330,15 @@
             dma((2,)),
         ],
         compiler_params=pltpu.CompilerParams(
-            collective_id=0, has_side_effects=True, vmem_limit_bytes=48 * 2**20
+            collective_id=0, has_side_effects=True, vmem_limit_bytes=67043328
         ),
         name="exchange_and_check",
     )(
-        trajectory, weights, observed, window, block, counts, flags,
-        inv_error.reshape(1, levels),
+        trajectory, weights, observed, window.reshape(1, groups), block.reshape(1, groups),
+        counts.reshape(1, groups), flags, inv_error.reshape(1, levels),
     )
+    plus_one = sums[2:3] + 1.0
+    return departures, sums[0:1] / jnp.sqrt(plus_one), sums[1:2] / plus_one
 
 
 def solution(mesh):

time: 111 us -> 105 us (0.946)
  local copies, waits for them, and re-layouts: 9.46 us -> 2.31 us
  other arithmetic: 0 us -> 1.31 us
    unnamed x14 -> x1, local copies, waits for them, and re-layouts: 8.14 us -> 2.31 us
    pad x2 -> x0, local copies, waits for them, and re-layouts: 1.32 us -> none  [the longest x1 0.66 us: per_device(): block = jnp.pad(block.reshape(1, groups), pad)]
    div x0 -> x1, other arithmetic: none -> 1.31 us  [per_device(): return (departures, sums[0:1] / jnp.sqrt(plus_one), sums[1:2] / plus_one)]
where the time goes in v2:
time: 105 us
  Pallas kernels  101 us (96%)
  local copies, waits for them, and re-layouts  2.31 us (2%)
  other arithmetic  1.31 us (1%)
    pallas_call x1, Pallas kernels, per_device(): pl.pallas_call(kernel, out_shape=(jax.ShapeDtypeStruct((groups, slots, le...  101 us
    unnamed x1, local copies, waits for them, and re-layouts  2.31 us

profile of v2, /device:TPU:1, one launch (start us, length us, event | category | flops | bytes accessed | tf_op | source)
XLA Modules:
  0.0 104.9 jit_solution(15212805610992250965)
XLA Ops:
  0.6 100.7 %exchange_and_check.1 = (bf16[32,128,128]{2,1,0:T(8,128)(2,1)}, f32[8,128]{1,0:T(8,128)}) custom-call(bf16[1,16,256,128]{3,2,1,0:T(8,128)(2,1)} %traj.1, bf16[32,128,256]{2,1,0:T(8,128)(2,1)} %weights.1, bf16[32,128,128]{2,1,0:T(8,128)(2,1)} %observed.1, s32[1,32]{1,0:T(1,128)} %bitcast.4, s32[1,32]{1,0:T(1,128)} %bitcast.5, s32[1,32]{1,0:T(1,128)} %bitcast.6, ...), custom_call_target="tpu_custom_call" | custom-call | tf_op jit(solution)/shard_map/exchange_and_check/pallas_call | solution.py:294
  101.3 1.3 %slice_divide_fusion = (f32[1,128]{1,0:T(1,128)}, f32[1,128]{1,0:T(1,128)}) fusion(f32[8,128]{1,0:T(8,128)} %get-tuple-element.6), kind=kLoop, calls=%fused_computation | loop fusion | flops 384 | bytes 2560 | tf_op jit(solution)/shard_map/div | solution.py:341
  102.6 2.3 %copy.12 = bf16[32,128,128]{2,1,0:T(8,128)(2,1)} copy(bf16[32,128,128]{2,1,0:T(8,128)(2,1)} %get-tuple-element.12) | data formatting | bytes 2097152

commit v3 on v2

--- a/solution.py
+++ b/solution.py
@@ -9,37 +9,38 @@
 GCAP = 4
 PIECE = 2
 
-SLABS = ((0, 0), (-1, 0), (1, 0), (-2, 0), (2, 0))
-TABLE_TO = ((0, 1), (-1, 0), (-1, 1), (-2, 0), (1, 0), (1, 1), (2, 1))
+SLABS = ((0, 0), (-1, 0), (1, 0), (-2, 0), (2, 0), (2, 1))
+FLOWS = ((0, 1, 1, 0), (0, 2, -1, 0), (1, 3, 1, 0), (2, 4, -1, 0), (4, 5, 0, 1))
+PIECE_SEM = {0: 0, 1: 16 // PIECE, 3: 2 * (16 // PIECE)}
+TABLE_TO = ((0, 1), (-1, 0), (-1, 1), (-2, 0), (1, 0), (2, 0))
 PICKS = (
     (0, 1, 0, 0),
     (0, 1, 1, 0),
     (0, 1, 2, 0),
     (0, 1, 3, 0),
-    (0, 1, 4, 0),
     (1, 0, 3, 1),
     (1, 1, 3, 2),
     (2, 0, 3, 3),
     (-1, 0, 4, 4),
-    (-1, 1, 4, 5),
-    (-2, 1, 4, 6),
+    (-1, 0, 5, 4),
+    (-2, 0, 5, 5),
 )
 
 
 def kernel(
     traj, weights, observed, window, block, counts, flags, inv,
     dep_out, sums_out,
-    s0, s1, s2, s3, s4, picked, outgoing, w_all, y_all, deps, dep_rows, used_t,
+    s0, s1, s2, s3, s4, s5, picked, outgoing, w_all, y_all, deps, used_t,
     win_row, block_row, count_row, flag_rows, inv_vmem, my_table, tables,
     parts, from_tm, row_sum, from_obs, my_smem, far_smem,
-    load_sem, slab_send, slab_recv, pick_send, pick_recv, table_send, table_recv,
-    tm_send, tm_recv, obs_send, obs_recv, out_sem,
+    load_sem, slab_send, slab_recv, whole_recv, pick_send, pick_recv, table_send, table_recv,
+    tm_send, tm_recv, obs_send, obs_recv,
 ):
-    slabs = (s0, s1, s2, s3, s4)
+    slabs = (s0, s1, s2, s3, s4, s5)
     tm = lax.axis_index("tm")
     obs = lax.axis_index("obs")
     z, y = tm // 2, lax.rem(tm, 2)
-    n_tm, n_obs = 16, 16
+    n_obs = 16
     groups = 32
 
     def at(dz, dy):
@@ -47,10 +48,10 @@
 
     barrier = pltpu.get_barrier_semaphore()
 
+    for dz, dy in ((-1, 0), (1, 0), (0, 1)):
+        pl.semaphore_signal(barrier, 1, device_id={"tm": at(dz, dy)}, device_id_type=MESH)
+
     def greet(step, carry):
-        pl.semaphore_signal(
-            barrier, 1, device_id={"tm": lax.rem(tm + step, n_tm)}, device_id_type=MESH
-        )
         pl.semaphore_signal(
             barrier, 1, device_id={"obs": lax.rem(obs + step, n_obs)}, device_id_type=MESH
         )
@@ -92,27 +93,35 @@
     used_t[...] = jnp.transpose(used).astype(jnp.bfloat16)
 
     loads[0].wait()
-    pl.semaphore_wait(barrier, 2 * 15)
+    pl.semaphore_wait(barrier, 3 + 15)
 
     pieces = 16 // PIECE
 
     def slab_copy(flow, piece):
-        source, target, dz = ((s0, s1, 1), (s0, s2, -1), (s1, s3, 1), (s2, s4, -1))[flow]
+        source, target, dz, dy = FLOWS[flow]
         span = pl.ds(piece * PIECE, PIECE)
         return pltpu.make_async_remote_copy(
-            src_ref=source.at[span], dst_ref=target.at[span],
-            send_sem=slab_send.at[flow, piece], recv_sem=slab_recv.at[flow, piece],
-            device_id={"tm": at(dz, 0)}, device_id_type=MESH,
+            src_ref=slabs[source].at[span], dst_ref=slabs[target].at[span],
+            send_sem=slab_send.at[flow], recv_sem=slab_recv.at[PIECE_SEM[flow] + piece] if flow in PIECE_SEM else whole_recv.at[flow // 2 - 1],
+            device_id={"tm": at(dz, dy)}, device_id_type=MESH,
+        )
+
+    def all_of(flow):
+        source, target, dz, dy = FLOWS[flow]
+        return pltpu.make_async_remote_copy(
+            src_ref=slabs[source], dst_ref=slabs[target],
+            send_sem=slab_send.at[flow], recv_sem=whole_recv.at[max(flow // 2 - 1, 0)],
+            device_id={"tm": at(dz, dy)}, device_id_type=MESH,
         )
 
     def table_copy(k):
         return pltpu.make_async_remote_copy(
             src_ref=my_table, dst_ref=tables.at[k],
-            send_sem=table_send.at[k], recv_sem=table_recv.at[k],
+            send_sem=table_send.at[0], recv_sem=table_recv.at[k],
             device_id={"tm": at(*TABLE_TO[k])}, device_id_type=MESH,
         )
 
-    for k in range(len(TABLE_TO)):
+    for k in (1, 4, 0):
         table_copy(k).start()
     for piece in range(pieces):
         slab_copy(0, piece).start()
@@ -120,28 +129,29 @@
 
     to_smem = pltpu.make_async_copy(my_table, my_smem, load_sem.at[8])
     to_smem.start()
-    for k in range(len(TABLE_TO)):
-        table_copy(k).wait_recv()
-    far_to_smem = pltpu.make_async_copy(tables, far_smem, load_sem.at[9])
-    far_to_smem.start()
+    table_copy(0).wait_recv()
+    mate_to_smem = pltpu.make_async_copy(tables.at[0], far_smem.at[0], load_sem.at[9])
+    mate_to_smem.start()
     to_smem.wait()
-    far_to_smem.wait()
+    mate_to_smem.wait()
 
     def pick_copy(m):
         dz, dy, _, _ = PICKS[m]
         return pltpu.make_async_remote_copy(
             src_ref=outgoing.at[m], dst_ref=picked.at[m],
-            send_sem=pick_send.at[m], recv_sem=pick_recv.at[m],
+            send_sem=pick_send.at[0], recv_sem=pick_recv.at[m],
             device_id={"tm": at(dz, dy)}, device_id_type=MESH,
         )
 
-    def pick(*numbers):
+    def pick(m):
+        _, _, slab, k = PICKS[m]
+        first = at(*SLABS[slab]) * GCAP
+        for r in range(GCAP):
+            outgoing[m, r] = slabs[slab][far_smem[k, 0, first + r]]
+
+    def send(*numbers):
         for m in numbers:
-            _, _, slab, k = PICKS[m]
-            first = at(*SLABS[slab]) * GCAP
-            for r in range(GCAP):
-                outgoing[m, r] = slabs[slab][far_smem[k, 0, first + r]]
-        for m in numbers:
+            pick(m)
             pick_copy(m).start()
 
     inv_row = inv_vmem[...]
@@ -151,7 +161,7 @@
     def part_copy(q, dz, dy):
         return pltpu.make_async_remote_copy(
             src_ref=parts.at[q], dst_ref=from_tm.at[q],
-            send_sem=tm_send.at[q], recv_sem=tm_recv.at[q],
+            send_sem=tm_send.at[0], recv_sem=tm_recv.at[0],
             device_id={"tm": at(dz, dy)}, device_id_type=MESH,
         )
 
@@ -195,55 +205,72 @@
 
     def compute_picked(m):
         dz, dy, slab, _ = PICKS[m]
-        compute(SLABS[slab][0] - dz, dy, lambda r, number: picked[m, r])
-
-    pick(0)
+        compute(SLABS[slab][0] - dz, dy ^ SLABS[slab][1], lambda r, number: picked[m, r])
+
+    def receive(m):
+        pick_copy(m).wait_recv()
+        compute_picked(m)
+
+    send(0)
     loads[1].wait()
     loads[2].wait()
     parts[...] = jnp.zeros_like(parts)
     compute_slab(0)
+    table_copy(1).wait_recv()
+    table_copy(4).wait_recv()
+    for k in (2, 3, 5):
+        table_copy(k).start()
 
     for piece in range(pieces):
         slab_copy(0, piece).wait_recv()
         slab_copy(2, piece).start()
         slab_copy(1, piece).wait_recv()
         slab_copy(3, piece).start()
-    pick(1, 2)
-    pick_copy(0).wait_recv()
-    compute_picked(0)
-    compute_slab(1)
-    compute_slab(2)
-    pick_copy(1).wait_recv()
-    compute_picked(1)
-    pick_copy(2).wait_recv()
-    compute_picked(2)
-
+    pick(1)
+    pick(2)
+    beside = [lambda: compute_slab(1), lambda: compute_slab(2), lambda: receive(0)]
     for piece in range(pieces):
-        slab_copy(2, piece).wait_recv()
         slab_copy(3, piece).wait_recv()
-    pick(6, 9, 7, 10, 5, 8)
-    pick(3, 4)
+        slab_copy(4, piece).start()
+        if beside:
+            beside.pop(0)()
+        if piece == pieces - 3:
+            for k in (2, 3, 5):
+                table_copy(k).wait_recv()
+            rest = pl.ds(1, len(TABLE_TO) - 1)
+            far_to_smem = pltpu.make_async_copy(
+                tables.at[rest], far_smem.at[rest], load_sem.at[10]
+            )
+            far_to_smem.start()
+    far_to_smem.wait()
+    pick_copy(1).start()
+    pick_copy(2).start()
+
+    all_of(2).wait_recv()
+    send(6, 7, 4, 5, 3)
     compute_slab(3)
     compute_slab(4)
-    for m in (6, 9, 7, 10, 5, 8, 3, 4):
-        pick_copy(m).wait_recv()
-        compute_picked(m)
+    all_of(4).wait_recv()
+    send(9, 8)
+    compute_slab(5)
+    for m in (1, 7, 6, 2, 3, 9, 4, 8, 5):
+        receive(m)
+
+    others = pl.ds(1, 15)
+
+    def wait_bytes(ref, semaphore):
+        pltpu.make_async_copy(ref, ref, semaphore).wait()
 
     def put(lo, hi):
         for g in range(lo, hi):
-            dep_rows[g] = deps[my_smem[2, g]]
-
-    def out_copy(lo, size):
-        span = pl.ds(lo, size)
-        return pltpu.make_async_copy(dep_rows.at[span], dep_out.at[span], out_sem.at[lo // size])
+            dep_out[g] = deps[my_smem[2, g]]
 
     put(0, 4)
     send_part()
     put(4, 16)
-    out_copy(0, 16).start()
     total = parts[0]
-    for q, dz, dy in done[1:]:
-        part_copy(q, dz, dy).wait_recv()
+    wait_bytes(from_tm.at[others], tm_recv.at[0])
+    for q in range(1, 16):
         total = total + from_tm[q]
     row_sum[...] = total
     put(16, 20)
@@ -251,33 +278,25 @@
     def obs_copy(step):
         return pltpu.make_async_remote_copy(
             src_ref=row_sum, dst_ref=from_obs.at[step],
-            send_sem=obs_send.at[step], recv_sem=obs_recv.at[step],
+            send_sem=obs_send.at[0], recv_sem=obs_recv.at[0],
             device_id={"obs": lax.rem(obs + step, n_obs)}, device_id_type=MESH,
         )
 
     for step in range(1, n_obs):
         obs_copy(step).start()
     put(20, 32)
-    out_copy(16, 16).start()
-
-    for piece in range(pieces):
-        for flow in range(4):
-            slab_copy(flow, piece).wait_send()
-    for k in range(len(TABLE_TO)):
-        table_copy(k).wait_send()
-    for m in range(len(PICKS)):
-        pick_copy(m).wait_send()
-    for q, dz, dy in done[1:]:
-        part_copy(q, dz, dy).wait_send()
-
+
+    for flow in range(len(FLOWS)):
+        all_of(flow).wait_send()
+    wait_bytes(tables, table_send.at[0])
+    wait_bytes(outgoing, pick_send.at[0])
+    wait_bytes(from_tm.at[others], tm_send.at[0])
+
+    wait_bytes(from_obs.at[others], obs_recv.at[0])
     for step in range(1, n_obs):
-        obs_copy(step).wait_recv()
         total = total + from_obs[step]
     sums_out[...] = total
-    for step in range(1, n_obs):
-        obs_copy(step).wait_send()
-    out_copy(0, 16).wait()
-    out_copy(16, 16).wait()
+    wait_bytes(from_obs.at[others], obs_send.at[0])
 
 
 def per_device(trajectory, weights, observed, window, block, counts, flags, inv_error):
@@ -291,6 +310,10 @@
     any_space = pl.BlockSpec(memory_space=pl.ANY)
     vmem = pl.BlockSpec(memory_space=pltpu.VMEM)
     slab = pltpu.VMEM((blocks, columns, levels), bf16)
+    arrays = (
+        trajectory, weights, observed, window.reshape(1, groups), block.reshape(1, groups),
+        counts.reshape(1, groups), flags, inv_error.reshape(1, levels),
+    )
     departures, sums = pl.pallas_call(
         kernel,
         out_shape=(
@@ -298,15 +321,14 @@
             jax.ShapeDtypeStruct((8, levels), f32),
         ),
         in_specs=[any_space] * 8,
-        out_specs=(any_space, vmem),
+        out_specs=(vmem, vmem),
         scratch_shapes=[
-            slab, slab, slab, slab, slab,
+            slab, slab, slab, slab, slab, slab,
             pltpu.VMEM((picks, GCAP, columns, levels), bf16),
             pltpu.VMEM((picks, GCAP, columns, levels), bf16),
             pltpu.VMEM((groups, slots, columns), bf16),
             pltpu.VMEM((groups, slots, levels), bf16),
             pltpu.VMEM((16 * GCAP, slots, levels), bf16),
-            pltpu.VMEM((groups, slots, levels), bf16),
             pltpu.VMEM((slots, groups), bf16),
             pltpu.VMEM((1, groups), i32),
             pltpu.VMEM((1, groups), i32),
@@ -321,22 +343,18 @@
             pltpu.VMEM((16, 8, levels), f32),
             pltpu.SMEM((8, 128), i32),
             pltpu.SMEM((tables, 8, 128), i32),
-            dma((10,)),
-            dma((4, pieces)), dma((4, pieces)),
-            dma((picks,)), dma((picks,)),
-            dma((tables,)), dma((tables,)),
-            dma((16,)), dma((16,)),
-            dma((16,)), dma((16,)),
-            dma((2,)),
+            dma((11,)),
+            dma((len(FLOWS),)), dma((3 * pieces,)), dma((2,)),
+            dma((1,)), dma((picks,)),
+            dma((1,)), dma((tables,)),
+            dma((1,)), dma((1,)),
+            dma((1,)), dma((1,)),
         ],
         compiler_params=pltpu.CompilerParams(
-            collective_id=0, has_side_effects=True, vmem_limit_bytes=67043328
+            collective_id=0, has_side_effects=True, vmem_limit_bytes=40 * 2**20
         ),
         name="exchange_and_check",
-    )(
-        trajectory, weights, observed, window.reshape(1, groups), block.reshape(1, groups),
-        counts.reshape(1, groups), flags, inv_error.reshape(1, levels),
-    )
+    )(*(pltpu.with_memory_space_constraint(array, pltpu.HBM) for array in arrays))
     plus_one = sums[2:3] + 1.0
     return departures, sums[0:1] / jnp.sqrt(plus_one), sums[1:2] / plus_one
 

time: 105 us -> 101 us (0.962)
  Pallas kernels: 101 us -> 98.5 us
  local copies, waits for them, and re-layouts: 2.31 us -> 0.97 us
    pallas_call x1, Pallas kernels: 101 us -> 98.5 us  [per_device(): pl.pallas_call(kernel, out_shape=(jax.ShapeDtypeStruct((groups, slots, le...]
    unnamed x1, local copies, waits for them, and re-layouts: 2.31 us -> 0.97 us
where the time goes in v3:
time: 101 us
  Pallas kernels  98.5 us (98%)
    pallas_call x1, Pallas kernels, per_device(): pl.pallas_call(kernel, out_shape=(jax.ShapeDtypeStruct((groups, slots, le...  98.5 us

profile of v3, /device:TPU:1, one launch (start us, length us, event | category | flops | bytes accessed | tf_op | source)
XLA Modules:
  0.0 100.6 jit_solution(16772963256353356695)
XLA Ops:
  0.6 98.5 %exchange_and_check.1 = (bf16[32,128,128]{2,1,0:T(8,128)(2,1)S(1)}, f32[8,128]{1,0:T(8,128)S(1)}) custom-call(bf16[1,16,256,128]{3,2,1,0:T(8,128)(2,1)} %traj.1, bf16[32,128,256]{2,1,0:T(8,128)(2,1)} %weights.1, bf16[32,128,128]{2,1,0:T(8,128)(2,1)} %observed.1, s32[1,32]{1,0:T(1,128)} %bitcast.4, s32[1,32]{1,0:T(1,128)} %bitcast.5, s32[1,32]{1,0:T(1,128)} %bitcast.6, ...), custom_call_target="tpu_custom_call" | custom-call | tf_op jit(solution)/shard_map/exchange_and_check/pallas_call | solution.py:317
  99.1 0.5 slice_divide_fusion
  99.7 1.0 copy.12

commit v4 on v3

--- a/solution.py
+++ b/solution.py
@@ -8,6 +8,8 @@
 MESH = pl.DeviceIdType.MESH
 GCAP = 4
 PIECE = 2
+AHEAD = 3
+LATE = 2
 
 SLABS = ((0, 0), (-1, 0), (1, 0), (-2, 0), (2, 0), (2, 1))
 FLOWS = ((0, 1, 1, 0), (0, 2, -1, 0), (1, 3, 1, 0), (2, 4, -1, 0), (4, 5, 0, 1))
@@ -32,9 +34,9 @@
     dep_out, sums_out,
     s0, s1, s2, s3, s4, s5, picked, outgoing, w_all, y_all, deps, used_t,
     win_row, block_row, count_row, flag_rows, inv_vmem, my_table, tables,
-    parts, from_tm, row_sum, from_obs, my_smem, far_smem,
+    parts, from_tm, row_sum, from_obs, from_late, my_smem, far_smem,
     load_sem, slab_send, slab_recv, whole_recv, pick_send, pick_recv, table_send, table_recv,
-    tm_send, tm_recv, obs_send, obs_recv,
+    tm_send, tm_recv, obs_send, obs_recv, late_send, late_recv,
 ):
     slabs = (s0, s1, s2, s3, s4, s5)
     tm = lax.axis_index("tm")
@@ -125,7 +127,8 @@
         table_copy(k).start()
     for piece in range(pieces):
         slab_copy(0, piece).start()
-        slab_copy(1, piece).start()
+        if piece < AHEAD:
+            slab_copy(1, piece).start()
 
     to_smem = pltpu.make_async_copy(my_table, my_smem, load_sem.at[8])
     to_smem.start()
@@ -157,17 +160,28 @@
     inv_row = inv_vmem[...]
     group_ids = lax.broadcasted_iota(jnp.int32, (groups, 128), 0)
     done = []
+    rows = pl.ds(0, 4)
 
     def part_copy(q, dz, dy):
         return pltpu.make_async_remote_copy(
-            src_ref=parts.at[q], dst_ref=from_tm.at[q],
+            src_ref=parts.at[q, rows], dst_ref=from_tm.at[q, rows],
             send_sem=tm_send.at[0], recv_sem=tm_recv.at[0],
             device_id={"tm": at(dz, dy)}, device_id_type=MESH,
         )
 
+    def late_copy(q, dz, dy, step):
+        return pltpu.make_async_remote_copy(
+            src_ref=parts.at[q, rows], dst_ref=from_late.at[q - (16 - LATE), step, rows],
+            send_sem=late_send.at[0], recv_sem=late_recv.at[0],
+            device_id={"tm": at(dz, dy), "obs": lax.rem(obs + step, n_obs)}, device_id_type=MESH,
+        )
+
     def send_part():
         q, dz, dy = done[-1]
-        if q > 0:
+        if q >= 16 - LATE:
+            for step in range(n_obs):
+                late_copy(q, dz, dy, step).start()
+        elif q > 0:
             part_copy(q, dz, dy).start()
 
     def compute(dz, dy, block_of):
@@ -211,40 +225,63 @@
         pick_copy(m).wait_recv()
         compute_picked(m)
 
+    def forward_up(*numbers):
+        for piece in numbers:
+            slab_copy(0, piece).wait_recv()
+            slab_copy(2, piece).start()
+
+    def forward_down(piece):
+        slab_copy(1, piece).wait_recv()
+        slab_copy(3, piece).start()
+        if piece + AHEAD < pieces:
+            slab_copy(1, piece + AHEAD).start()
+
+    def cross(piece):
+        slab_copy(3, piece).wait_recv()
+        slab_copy(4, piece).start()
+
     send(0)
+    forward_down(0)
     loads[1].wait()
     loads[2].wait()
     parts[...] = jnp.zeros_like(parts)
     compute_slab(0)
+    forward_down(1)
     table_copy(1).wait_recv()
     table_copy(4).wait_recv()
     for k in (2, 3, 5):
         table_copy(k).start()
-
-    for piece in range(pieces):
-        slab_copy(0, piece).wait_recv()
-        slab_copy(2, piece).start()
-        slab_copy(1, piece).wait_recv()
-        slab_copy(3, piece).start()
-    pick(1)
-    pick(2)
-    beside = [lambda: compute_slab(1), lambda: compute_slab(2), lambda: receive(0)]
-    for piece in range(pieces):
-        slab_copy(3, piece).wait_recv()
-        slab_copy(4, piece).start()
-        if beside:
-            beside.pop(0)()
-        if piece == pieces - 3:
-            for k in (2, 3, 5):
-                table_copy(k).wait_recv()
-            rest = pl.ds(1, len(TABLE_TO) - 1)
-            far_to_smem = pltpu.make_async_copy(
-                tables.at[rest], far_smem.at[rest], load_sem.at[10]
-            )
-            far_to_smem.start()
+    forward_up(0, 1)
+    forward_down(2)
+    forward_up(2)
+    cross(0)
+    forward_up(3)
+    forward_down(3)
+    forward_up(4)
+    cross(1)
+    forward_up(5)
+    forward_down(4)
+    forward_up(6, 7)
+    send(1)
+    cross(2)
+    compute_slab(1)
+    forward_down(5)
+    receive(0)
+    cross(3)
+    forward_down(6)
+    cross(4)
+    forward_down(7)
+    send(2)
+    compute_slab(2)
+    cross(5)
+    for k in (2, 3, 5):
+        table_copy(k).wait_recv()
+    rest = pl.ds(1, len(TABLE_TO) - 1)
+    far_to_smem = pltpu.make_async_copy(tables.at[rest], far_smem.at[rest], load_sem.at[10])
+    far_to_smem.start()
+    cross(6)
+    cross(7)
     far_to_smem.wait()
-    pick_copy(1).start()
-    pick_copy(2).start()
 
     all_of(2).wait_recv()
     send(6, 7, 4, 5, 3)
@@ -253,10 +290,11 @@
     all_of(4).wait_recv()
     send(9, 8)
     compute_slab(5)
-    for m in (1, 7, 6, 2, 3, 9, 4, 8, 5):
+    for m in (1, 2, 7, 3, 6, 9, 4, 8, 5):
         receive(m)
 
     others = pl.ds(1, 15)
+    early = pl.ds(1, 15 - LATE)
 
     def wait_bytes(ref, semaphore):
         pltpu.make_async_copy(ref, ref, semaphore).wait()
@@ -269,15 +307,15 @@
     send_part()
     put(4, 16)
     total = parts[0]
-    wait_bytes(from_tm.at[others], tm_recv.at[0])
-    for q in range(1, 16):
+    wait_bytes(from_tm.at[early, rows], tm_recv.at[0])
+    for q in range(1, 16 - LATE):
         total = total + from_tm[q]
     row_sum[...] = total
     put(16, 20)
 
     def obs_copy(step):
         return pltpu.make_async_remote_copy(
-            src_ref=row_sum, dst_ref=from_obs.at[step],
+            src_ref=row_sum.at[rows], dst_ref=from_obs.at[step, rows],
             send_sem=obs_send.at[0], recv_sem=obs_recv.at[0],
             device_id={"obs": lax.rem(obs + step, n_obs)}, device_id_type=MESH,
         )
@@ -290,13 +328,18 @@
         all_of(flow).wait_send()
     wait_bytes(tables, table_send.at[0])
     wait_bytes(outgoing, pick_send.at[0])
-    wait_bytes(from_tm.at[others], tm_send.at[0])
-
-    wait_bytes(from_obs.at[others], obs_recv.at[0])
+    wait_bytes(from_tm.at[early, rows], tm_send.at[0])
+
+    wait_bytes(from_obs.at[others, rows], obs_recv.at[0])
     for step in range(1, n_obs):
         total = total + from_obs[step]
+    wait_bytes(from_late.at[pl.ds(0, LATE), pl.ds(0, n_obs), rows], late_recv.at[0])
+    for number in range(LATE):
+        for step in range(n_obs):
+            total = total + from_late[number, step]
     sums_out[...] = total
-    wait_bytes(from_obs.at[others], obs_send.at[0])
+    wait_bytes(from_obs.at[others, rows], obs_send.at[0])
+    wait_bytes(from_late.at[pl.ds(0, LATE), pl.ds(0, n_obs), rows], late_send.at[0])
 
 
 def per_device(trajectory, weights, observed, window, block, counts, flags, inv_error):
@@ -341,12 +384,14 @@
             pltpu.VMEM((16, 8, levels), f32),
             pltpu.VMEM((8, levels), f32),
             pltpu.VMEM((16, 8, levels), f32),
+            pltpu.VMEM((LATE, 16, 8, levels), f32),
             pltpu.SMEM((8, 128), i32),
             pltpu.SMEM((tables, 8, 128), i32),
             dma((11,)),
             dma((len(FLOWS),)), dma((3 * pieces,)), dma((2,)),
             dma((1,)), dma((picks,)),
             dma((1,)), dma((tables,)),
+            dma((1,)), dma((1,)),
             dma((1,)), dma((1,)),
             dma((1,)), dma((1,)),
         ],

time: 101 us -> 94.4 us (0.935)
  Pallas kernels: 98.5 us -> 92.2 us
    pallas_call x1, Pallas kernels: 98.5 us -> 92.2 us  [per_device(): pl.pallas_call(kernel, out_shape=(jax.ShapeDtypeStruct((groups, slots, le...]
where the time goes in v4:
time: 94.4 us; the launch traced here: 94.3 us
  Pallas kernels  92.2 us (98%)
  local copies, waits for them, and re-layouts  0.97 us (1%)
    pallas_call x1, Pallas kernels, per_device(): pl.pallas_call(kernel, out_shape=(jax.ShapeDtypeStruct((groups, slots, le...  92.2 us

profile of v4, /device:TPU:1, one launch (start us, length us, event | category | flops | bytes accessed | tf_op | source)
XLA Modules:
  0.0 94.3 jit_solution(13966383113876250376)
XLA Ops:
  0.6 92.2 %exchange_and_check.1 = (bf16[32,128,128]{2,1,0:T(8,128)(2,1)S(1)}, f32[8,128]{1,0:T(8,128)S(1)}) custom-call(bf16[1,16,256,128]{3,2,1,0:T(8,128)(2,1)} %traj.1, bf16[32,128,256]{2,1,0:T(8,128)(2,1)} %weights.1, bf16[32,128,128]{2,1,0:T(8,128)(2,1)} %observed.1, s32[1,32]{1,0:T(1,128)} %bitcast.4, s32[1,32]{1,0:T(1,128)} %bitcast.5, s32[1,32]{1,0:T(1,128)} %bitcast.6, ...), custom_call_target="tpu_custom_call" | custom-call | tf_op jit(solution)/shard_map/exchange_and_check/pallas_call | solution.py:360
  92.8 0.5 slice_divide_fusion
  93.3 1.0 %copy.12 = bf16[32,128,128]{2,1,0:T(8,128)(2,1)} copy(bf16[32,128,128]{2,1,0:T(8,128)(2,1)S(1)} %get-tuple-element.12) | data formatting | bytes 2097152

commit v5 on v4

--- a/solution.py
+++ b/solution.py
@@ -69,10 +69,10 @@
         pltpu.make_async_copy(source, target, load_sem.at[n])
         for n, (source, target) in enumerate(pairs)
     ]
-    for load in loads[3:] + loads[:3]:
+    for load in loads[3:5] + loads[:1] + loads[5:] + loads[1:3]:
         load.start()
 
-    for load in loads[3:]:
+    for load in loads[3:5]:
         load.wait()
     lane = lax.broadcasted_iota(jnp.int32, (groups, groups), 1)
     row = lax.broadcasted_iota(jnp.int32, (groups, groups), 0)
@@ -91,8 +91,6 @@
     my_table[0:1, :] = jnp.sum(jnp.where(hit, turned(block_row), 0), 0, keepdims=True)
     my_table[1:2, :] = jnp.sum(jnp.where(hit, wide_row + 1, 0), 0, keepdims=True) - 1
     my_table[2:3, 0:groups] = win_row[...] * GCAP + rank_row
-    used = jnp.where(wide_lane < turned(count_row), flag_rows[...], 0).astype(jnp.float32)
-    used_t[...] = jnp.transpose(used).astype(jnp.bfloat16)
 
     loads[0].wait()
     pl.semaphore_wait(barrier, 3 + 15)
@@ -130,6 +128,10 @@
         if piece < AHEAD:
             slab_copy(1, piece).start()
 
+    for load in loads[5:]:
+        load.wait()
+    used = jnp.where(wide_lane < turned(count_row), flag_rows[...], 0).astype(jnp.float32)
+    used_t[...] = jnp.transpose(used).astype(jnp.bfloat16)
     to_smem = pltpu.make_async_copy(my_table, my_smem, load_sem.at[8])
     to_smem.start()
     table_copy(0).wait_recv()
@@ -290,7 +292,7 @@
     all_of(4).wait_recv()
     send(9, 8)
     compute_slab(5)
-    for m in (1, 2, 7, 3, 6, 9, 4, 8, 5):
+    for m in (1, 2, 7, 6, 3, 9, 4, 5, 8):
         receive(m)
 
     others = pl.ds(1, 15)

time: 94.4 us -> 93.3 us (0.988)
  Pallas kernels: 92.2 us -> 91 us
    pallas_call x1, Pallas kernels: 92.2 us -> 91 us  [per_device(): pl.pallas_call(kernel, out_shape=(jax.ShapeDtypeStruct((groups, slots, le...]
where the time goes in v5:
time: 93.3 us; the launch traced here: 93.1 us
  Pallas kernels  91 us (98%)
  local copies, waits for them, and re-layouts  0.97 us (1%)
    pallas_call x1, Pallas kernels, per_device(): pl.pallas_call(kernel, out_shape=(jax.ShapeDtypeStruct((groups, slots, le...  91 us

profile of v5, /device:TPU:1, one launch (start us, length us, event | category | flops | bytes accessed | tf_op | source)
XLA Modules:
  0.0 93.1 jit_solution(3533804105411446867)
XLA Ops:
  0.6 91.0 %exchange_and_check.1 = (bf16[32,128,128]{2,1,0:T(8,128)(2,1)S(1)}, f32[8,128]{1,0:T(8,128)S(1)}) custom-call(bf16[1,16,256,128]{3,2,1,0:T(8,128)(2,1)} %traj.1, bf16[32,128,256]{2,1,0:T(8,128)(2,1)} %weights.1, bf16[32,128,128]{2,1,0:T(8,128)(2,1)} %observed.1, s32[1,32]{1,0:T(1,128)} %bitcast.4, s32[1,32]{1,0:T(1,128)} %bitcast.5, s32[1,32]{1,0:T(1,128)} %bitcast.6, ...), custom_call_target="tpu_custom_call" | custom-call | tf_op jit(solution)/shard_map/exchange_and_check/pallas_call | solution.py:362
  91.6 0.5 slice_divide_fusion
  92.1 1.0 %copy.12 = bf16[32,128,128]{2,1,0:T(8,128)(2,1)} copy(bf16[32,128,128]{2,1,0:T(8,128)(2,1)S(1)} %get-tuple-element.12) | data formatting | bytes 2097152

commit v6 on v5

--- a/solution.py
+++ b/solution.py
@@ -207,7 +207,7 @@
             return one, two, kept
 
         zero = jnp.zeros((8, 128), jnp.float32)
-        one, two, kept = lax.fori_loop(0, GCAP, body, (zero, zero, zero))
+        one, two, kept = lax.fori_loop(0, GCAP, body, (zero, zero, zero), unroll=True)
         parts[q, 0:1, :] = jnp.sum(one, 0, keepdims=True)
         parts[q, 1:2, :] = jnp.sum(two, 0, keepdims=True)
         parts[q, 2:3, :] = jnp.sum(kept, 0, keepdims=True)

time: 93.3 us -> 93.1 us (level)
  no operation moved by 1% of the time
where the time goes in v6:
time: 93.1 us; the launch traced here: 92.7 us
  Pallas kernels  90.5 us (97%)
  local copies, waits for them, and re-layouts  0.97 us (1%)
    pallas_call x1, Pallas kernels, per_device(): pl.pallas_call(kernel, out_shape=(jax.ShapeDtypeStruct((groups, slots, le...  90.5 us

profile of v6, /device:TPU:1, one launch (start us, length us, event | category | flops | bytes accessed | tf_op | source)
XLA Modules:
  0.0 92.7 jit_solution(11243306627844497422)
XLA Ops:
  0.6 90.5 %exchange_and_check.1 = (bf16[32,128,128]{2,1,0:T(8,128)(2,1)S(1)}, f32[8,128]{1,0:T(8,128)S(1)}) custom-call(bf16[1,16,256,128]{3,2,1,0:T(8,128)(2,1)} %traj.1, bf16[32,128,256]{2,1,0:T(8,128)(2,1)} %weights.1, bf16[32,128,128]{2,1,0:T(8,128)(2,1)} %observed.1, s32[1,32]{1,0:T(1,128)} %bitcast.4, s32[1,32]{1,0:T(1,128)} %bitcast.5, s32[1,32]{1,0:T(1,128)} %bitcast.6, ...), custom_call_target="tpu_custom_call" | custom-call | tf_op jit(solution)/shard_map/exchange_and_check/pallas_call | solution.py:362
  91.2 0.5 slice_divide_fusion
  91.7 1.0 %copy.12 = bf16[32,128,128]{2,1,0:T(8,128)(2,1)} copy(bf16[32,128,128]{2,1,0:T(8,128)(2,1)S(1)} %get-tuple-element.12) | data formatting | bytes 2097152
